TPU v7x, 32 devices: a whole 2x2x4 slice. The times are simulated.
32 devices in a mesh: groups: 2 (over x), tm: 8 (over z, y), sector: 2 (over core).
Axes of the slice: x: 2, y: 2, z: 4, core: 2. Of those that a mesh axis runs over, the one named last changes fastest.
Arguments:
- context: bfloat16 [16, 2, 512, 256], P(('groups', 'tm'), 'sector'), parts along dimension 0, may hold values from -6 to 6
- depth_weight: float32 [16, 2, 16, 512], P(('groups', 'tm'), 'sector'), parts along dimension 0, may hold values from 0 to 1
- cell_ids: int32 [2, 16, 512], P('sector'), may hold values from 0 to 4095
- time_embed: bfloat16 [8, 256], replicated, may hold values from -3 to 3
- norm_gain: float32 [2, 2, 256], replicated, may hold values from 0.1 to 1.9
- w_qkv: bfloat16 [2, 256, 768], replicated, may hold values from -15 to 15
- w_out: bfloat16 [2, 256, 256], replicated, may hold values from -0.375 to 0.375
- w_up: bfloat16 [2, 256, 1024], replicated, may hold values from -0.375 to 0.375
- w_down: bfloat16 [2, 1024, 256], replicated, may hold values from -0.1875 to 0.1875
- conv_weight: bfloat16 [3, 3, 256, 256], replicated, may hold values from -0.125 to 0.125
Outputs:
- bev_out: bfloat16 [16, 64, 64, 256], P(('groups', 'tm'), 'sector'), parts along dimension 0
There are 2 independent parts, one for each index of `groups`. A program takes and returns all parts, laid end to end along the dimension named above; an argument that names none is the same for every part. Nothing has to cross between parts.
All inputs are finite; a program needn't handle non-finite values.
Results may differ from a plain program's by a relative error of at most 0.0079.
Values may be sent and summed in bfloat16 or wider, within the bound.
No kernel may reach another device: no remote copies, remote signals or barrier semaphores. Data moves between devices by JAX's collectives and lax.ppermute only.
A program may use at most 128 MiB of HBM per device.

v0:
```python
import jax
import jax.numpy as jnp
from jax import lax
from jax.sharding import PartitionSpec as P

HEADS = 8
GRID = 64


def padded_2(cells, sides, width):
    for axis, dim in sides:
        count = lax.axis_size(axis)
        ends = count - 1
        head = lax.slice_in_dim(cells, 0, width, axis=dim)
        tail = lax.slice_in_dim(cells, cells.shape[dim] - width, cells.shape[dim], axis=dim)
        cells = jnp.concatenate(
            [
                lax.ppermute(tail, axis, [(i, (i + 1) % count) for i in range(ends)]),
                cells,
                lax.ppermute(head, axis, [((i + 1) % count, i) for i in range(ends)]),
            ],
            axis=dim,
        )
    return cells


def pool_local(context, depth_weight, cell_ids):
    cell_count = GRID * GRID
    block_cells = min(512, cell_count)
    cell_index = cell_ids[0]

    def one_frame(frame_inputs):
        features, weights = frame_inputs

        def one_block(first_cell):
            target = first_cell + lax.broadcasted_iota(jnp.int32, (block_cells, 1), 0)
            matches = cell_index[:, None, :] == target[None]
            matrix = jnp.sum(
                jnp.where(matches, weights[:, None, :], jnp.zeros_like(weights[:, None, :])), axis=0
            ).astype(jnp.bfloat16)
            return jnp.dot(matrix, features, preferred_element_type=jnp.float32).astype(
                jnp.bfloat16
            )

        starts = jnp.arange(cell_count // block_cells) * block_cells
        return lax.map(one_block, starts).reshape(cell_count, features.shape[-1])

    return lax.map(one_frame, (context[:, 0], depth_weight[:, 0]))


def normalize(values, gain):
    return values * lax.rsqrt(jnp.mean(values * values, axis=-1, keepdims=True) + 1e-05) * gain


def encode_stack(tokens, time_embed, norm_gain, w_qkv, w_out, w_up, w_down):
    frame_count, cell_count, channels = tokens.shape
    head_size = channels // HEADS
    query_frame = lax.broadcasted_iota(jnp.int32, (frame_count, frame_count), 0)
    key_frame = lax.broadcasted_iota(jnp.int32, (frame_count, frame_count), 1)
    allowed = key_frame <= query_frame
    stream = (tokens.astype(jnp.float32) + time_embed[:, None, :].astype(jnp.float32)).reshape(
        frame_count * cell_count, channels
    )
    for number in range(w_qkv.shape[0]):
        normed = normalize(stream, norm_gain[number, 0]).astype(jnp.bfloat16)
        projected = jnp.dot(normed, w_qkv[number], preferred_element_type=jnp.float32).astype(
            jnp.bfloat16
        )
        projected = projected.reshape(frame_count, cell_count, 3, HEADS, head_size)
        scores = jnp.einsum(
            "fchd,gchd->chfg",
            projected[:, :, 0],
            projected[:, :, 1],
            preferred_element_type=jnp.float32,
        ) * head_size ** (-0.5)
        scores = jnp.where(allowed, scores, -1e30)
        largest = jnp.max(scores, axis=-1, keepdims=True)
        raised = jnp.exp(scores - largest)
        soft_weights = (raised / jnp.sum(raised, axis=-1, keepdims=True)).astype(jnp.bfloat16)
        mixed = jnp.einsum(
            "chfg,gchd->fchd", soft_weights, projected[:, :, 2], preferred_element_type=jnp.float32
        ).astype(jnp.bfloat16)
        mixed = mixed.reshape(frame_count * cell_count, channels)
        stream = stream + jnp.dot(mixed, w_out[number], preferred_element_type=jnp.float32)
        normed_second = normalize(stream, norm_gain[number, 1]).astype(jnp.bfloat16)
        hidden_units = jax.nn.gelu(
            jnp.dot(normed_second, w_up[number], preferred_element_type=jnp.float32),
            approximate=True,
        ).astype(jnp.bfloat16)
        stream = stream + jnp.dot(hidden_units, w_down[number], preferred_element_type=jnp.float32)
    return stream.reshape(frame_count, cell_count, channels).astype(jnp.bfloat16)


def encode_return(tokens, weights):
    encoded = encode_stack(tokens, *weights)
    return lax.all_to_all(encoded, "tm", split_axis=0, concat_axis=1, tiled=True)


def body(
    context, depth_weight, cell_ids, time_embed, norm_gain, w_qkv, w_out, w_up, w_down, conv_weight
):
    partial_value = lax.optimization_barrier(pool_local(context, depth_weight, cell_ids))
    frames_dev, cell_count, channels = partial_value.shape
    tm_count = lax.axis_size("tm")
    band_cells = cell_count // lax.axis_size("sector")
    piece_cells = band_cells // tm_count
    weights = (time_embed, norm_gain, w_qkv, w_out, w_up, w_down)
    pooled = (
        lax.psum_scatter(partial_value, "sector", scatter_dimension=1, tiled=True)
        .astype(jnp.float32)
        .astype(jnp.bfloat16)
    )
    sectioned = pooled.reshape(frames_dev, tm_count, piece_cells, channels)
    received = lax.all_to_all(sectioned, "tm", split_axis=1, concat_axis=0, tiled=True)
    tokens = received.reshape(received.shape[0], received.shape[2], channels)
    returned = encode_return(tokens, weights)
    item_count = returned.shape[1] // tm_count
    result = returned.reshape(frames_dev, tm_count, item_count, channels)
    row_count = band_cells // GRID
    encoded = result.reshape(frames_dev, row_count, GRID, channels)
    padded = padded_2(encoded, (("sector", 1),), 1)
    padded = jnp.pad(padded, ((0, 0), (0, 0), (1, 1), (0, 0)))
    summed = encoded.astype(jnp.float32)
    for offset in range(3):
        row_strip = padded[:, offset : offset + row_count]
        stacked = jnp.concatenate(
            [row_strip[:, :, column : column + GRID] for column in range(3)], axis=-1
        )
        product = jnp.dot(
            stacked.reshape(frames_dev * row_count * GRID, 3 * channels),
            conv_weight[offset].reshape(3 * channels, channels),
            preferred_element_type=jnp.float32,
        )
        summed = summed + product.reshape(summed.shape)
    return summed.astype(jnp.bfloat16)


def solution(mesh):
    return jax.shard_map(
        body,
        mesh=mesh,
        in_specs=(
            P(("groups", "tm"), "sector", None, None),
            P(("groups", "tm"), "sector", None, None),
            P("sector", None, None),
            P(),
            P(),
            P(),
            P(),
            P(),
            P(),
            P(),
        ),
        out_specs=P(("groups", "tm"), "sector", None, None),
        check_vma=False,
    )
```

profile of v0, /device:TPU:0, one launch (start us, length us, event | category | flops | bytes accessed | tf_op | source)
XLA Modules:
  0.0 295.6 jit_solution(16586934135951967975)
XLA Ops:
  6.5 45.5 %while.17 = (s32[]{:T(128)}, bf16[8,512,256]{2,1,0:T(8,128)(2,1)}, s32[1,16,512]{2,1,0:T(8,128)}, s32[8]{0:T(128)S(1)}, f32[16,512]{1,0:T(8,128)}, /*index=5*/bf16[512,256]{1,0:T(8,128)(2,1)}, s32[]{:T(128)}) while((s32[]{:T(128)}, bf16[8,512,256]{2,1,0:T(8,128)(2,1)}, s32[1,16,512]{2,1,0:T(8,128)}, s32[8]{0:T(128)S(1)}, f32[16,512]{1,0:T(8,128)}, ...), condition=%wide.region_2.3_spmd, body=%wide.region_0.2_spmd.sunk | while | flops 146670080 | bytes 1643101 | solution.py:46
  13.4 2.5 select_reduce_fusion.2
  19.1 2.5 select_reduce_fusion.2
  24.8 2.5 select_reduce_fusion.2
  36.2 2.5 select_reduce_fusion.2
  52.0 12.6 %reduce-scatter.2.cloned.1.call-done = bf16[1,2048,256]{2,1,0:T(8,128)(2,1)} async-done(((bf16[1,4096,256]{2,1,0:T(8,128)(2,1)}), bf16[1,2048,256]{2,1,0:T(8,128)(2,1)}) %reduce-scatter.2.cloned.1.call-update) | async-done | bytes 1048592 | tf_op jit(solution)/shard_map/reduce_scatter | solution.py:109
  64.7 6.2 %all-to-all-start = ((bf16[1,8,256,256]{3,2,0,1:T(8,128)(2,1)}), bf16[1,8,256,256]{3,2,0,1:T(8,128)(2,1)S(1)}, u32[]{:S(2)}, u32[]{:S(2)}) async-start(bf16[1,8,256,256]{3,2,0,1:T(8,128)(2,1)} %bitcast.169), calls=%async_computation.1 | async-start | bytes 2097152 | tf_op jit(solution)/shard_map/all_to_all | solution.py:114
  70.9 26.0 %all-to-all-done = bf16[1,8,256,256]{3,2,0,1:T(8,128)(2,1)S(1)} async-done(((bf16[1,8,256,256]{3,2,0,1:T(8,128)(2,1)}), bf16[1,8,256,256]{3,2,0,1:T(8,128)(2,1)S(1)}, u32[]{:S(2)}, u32[]{:S(2)}) %all-to-all-start) | async-done | bytes 1048608 | tf_op jit(solution)/shard_map/all_to_all | solution.py:114
  99.9 3.0 %copy.55 = bf16[2048,768]{0,1:T(8,128)(2,1)} copy(bf16[2048,768]{1,0:T(8,128)(2,1)S(1)} %convolution_convert_fusion.2) | data formatting | bytes 6291456 | tf_op jit(solution)/shard_map/convert_element_type | solution.py:66
  102.9 3.0 %copy.75 = bf16[96,8,8,256]{3,2,1,0:T(8,128)(2,1)S(1)} copy(bf16[96,8,8,256]{3,1,2,0:T(8,128)(2,1)} %bitcast.155) | data formatting | bytes 6291456
  106.1 7.2 %copy.70 = bf16[8,256,1,8,32]{4,0,3,1,2:T(8,128)(2,1)} copy(bf16[8,256,1,8,32]{1,0,4,3,2:T(8,128)(2,1)S(1)} %get-tuple-element.69) | data formatting | bytes 2097152
  113.2 7.2 %copy.71 = bf16[8,256,1,8,32]{4,0,3,1,2:T(8,128)(2,1)} copy(bf16[8,256,1,8,32]{1,0,4,3,2:T(8,128)(2,1)S(1)} %get-tuple-element.70) | data formatting | bytes 2097152
  120.4 9.0 %fusion.26 = f32[256,8,8,8]{2,3,1,0:T(8,128)} fusion(bf16[8,256,1,8,32]{4,0,3,1,2:T(8,128)(2,1)} %copy.71, bf16[8,256,1,8,32]{4,0,3,1,2:T(8,128)(2,1)} %copy.70), kind=kOutput, calls=%fused_computation.31 | convolution fusion | flops 8388608 | bytes 2621440 | tf_op jit(solution)/shard_map/fchd,gchd->chfg/dot_general | solution.py:70
  129.4 6.4 %copy.59 = f32[256,8,8,8]{0,3,2,1:T(8,128)S(1)} copy(f32[256,8,8,8]{2,3,1,0:T(8,128)} %fusion.26) | data formatting | bytes 1048576 | tf_op jit(solution)/shard_map/fchd,gchd->chfg/dot_general | solution.py:70
  136.9 6.4 %copy.60 = bf16[256,8,8,8]{3,2,1,0:T(8,128)(2,1)} copy(bf16[256,8,8,8]{0,3,2,1:T(8,128)(2,1)S(1)} %divide_convert_fusion.1) | data formatting | bytes 524288 | tf_op jit(solution)/shard_map/convert_element_type | solution.py:79
  143.3 7.7 %copy.69 = bf16[8,256,1,8,32]{4,0,3,1,2:T(8,128)(2,1)} copy(bf16[8,256,1,8,32]{1,0,4,3,2:T(8,128)(2,1)S(1)} %get-tuple-element.68) | data formatting | bytes 2097152
  151.0 7.8 %convert_bitcast_fusion.1 = bf16[8,256,8,32]{3,0,2,1:T(8,128)(2,1)} fusion(bf16[256,8,8,8]{3,2,1,0:T(8,128)(2,1)} %copy.60, bf16[8,256,1,8,32]{4,0,3,1,2:T(8,128)(2,1)} %copy.69), kind=kOutput, calls=%fused_computation.37 | convolution fusion | flops 8912896 | bytes 2359296 | tf_op jit(solution)/shard_map/chfg,gchd->fchd/dot_general | solution.py:80
  158.8 6.0 %copy.61 = bf16[8,256,8,32]{1,0,3,2:T(8,128)(2,1)S(1)} copy(bf16[8,256,8,32]{3,0,2,1:T(8,128)(2,1)} %convert_bitcast_fusion.1) | data formatting | bytes 2097152 | tf_op jit(solution)/shard_map/convert_element_type | solution.py:82
  166.4 5.9 %multiply_reduce_fusion.1 = (f32[2048]{0:T(1024)S(1)}, f32[2048,256]{1,0:T(8,128)}) fusion(f32[2048,256]{1,0:T(8,128)S(1)} %get-tuple-element.89, bf16[2,1024,256]{2,1,0:T(8,128)(2,1)} %param.20, f32[256]{0:T(256)S(1)} %bitcast.179, f32[2048]{0:T(1024)S(1)} %add_rsqrt_fusion.2, bf16[2,256,1024]{2,1,0:T(8,128)(2,1)} %param.19), kind=kOutput, calls=%fused_computation.83 | convolution fusion | flops 2169501696 | bytes 7357440 | tf_op jit(solution)/shard_map/dot_general | solution.py:90
  172.3 2.7 convolution_convert_fusion.1
  175.0 3.1 %copy.62 = bf16[2048,768]{0,1:T(8,128)(2,1)} copy(bf16[2048,768]{1,0:T(8,128)(2,1)S(1)} %convolution_convert_fusion.1) | data formatting | bytes 6291456 | tf_op jit(solution)/shard_map/convert_element_type | solution.py:66
  178.2 3.0 %copy.77 = bf16[96,8,8,256]{3,2,1,0:T(8,128)(2,1)S(1)} copy(bf16[96,8,8,256]{3,1,2,0:T(8,128)(2,1)} %bitcast.156) | data formatting | bytes 6291456
  181.4 7.2 %copy.73 = bf16[8,256,1,8,32]{4,0,3,1,2:T(8,128)(2,1)} copy(bf16[8,256,1,8,32]{1,0,4,3,2:T(8,128)(2,1)S(1)} %get-tuple-element.66) | data formatting | bytes 2097152
  188.5 7.2 %copy.74 = bf16[8,256,1,8,32]{4,0,3,1,2:T(8,128)(2,1)} copy(bf16[8,256,1,8,32]{1,0,4,3,2:T(8,128)(2,1)S(1)} %get-tuple-element.67) | data formatting | bytes 2097152
  195.7 9.0 %fusion.21 = f32[256,8,8,8]{2,3,1,0:T(8,128)} fusion(bf16[8,256,1,8,32]{4,0,3,1,2:T(8,128)(2,1)} %copy.74, bf16[8,256,1,8,32]{4,0,3,1,2:T(8,128)(2,1)} %copy.73), kind=kOutput, calls=%fused_computation.26 | convolution fusion | flops 8388608 | bytes 2621440 | tf_op jit(solution)/shard_map/fchd,gchd->chfg/dot_general | solution.py:70
  204.7 6.4 %copy.66 = f32[256,8,8,8]{0,3,2,1:T(8,128)S(1)} copy(f32[256,8,8,8]{2,3,1,0:T(8,128)} %fusion.21) | data formatting | bytes 1048576 | tf_op jit(solution)/shard_map/fchd,gchd->chfg/dot_general | solution.py:70
  212.2 6.4 %copy.67 = bf16[256,8,8,8]{3,2,1,0:T(8,128)(2,1)} copy(bf16[256,8,8,8]{0,3,2,1:T(8,128)(2,1)S(1)} %divide_convert_fusion) | data formatting | bytes 524288 | tf_op jit(solution)/shard_map/convert_element_type | solution.py:79
  218.6 7.4 %copy.72 = bf16[8,256,1,8,32]{4,0,3,1,2:T(8,128)(2,1)} copy(bf16[8,256,1,8,32]{1,0,4,3,2:T(8,128)(2,1)S(1)} %get-tuple-element.65) | data formatting | bytes 2097152
  226.0 7.8 %convert_bitcast_fusion = bf16[8,256,8,32]{3,0,2,1:T(8,128)(2,1)} fusion(bf16[256,8,8,8]{3,2,1,0:T(8,128)(2,1)} %copy.67, bf16[8,256,1,8,32]{4,0,3,1,2:T(8,128)(2,1)} %copy.72), kind=kOutput, calls=%fused_computation.36 | convolution fusion | flops 8912896 | bytes 2359296 | tf_op jit(solution)/shard_map/chfg,gchd->fchd/dot_general | solution.py:80
  233.7 6.0 %copy.68 = bf16[8,256,8,32]{1,0,3,2:T(8,128)(2,1)S(1)} copy(bf16[8,256,8,32]{3,0,2,1:T(8,128)(2,1)} %convert_bitcast_fusion) | data formatting | bytes 2097152 | tf_op jit(solution)/shard_map/convert_element_type | solution.py:82
  242.0 5.6 %fusion.70 = bf16[2048,256]{1,0:T(8,128)(2,1)S(1)} fusion(f32[2048,256]{1,0:T(8,128)} %get-tuple-element.95, f32[256]{0:T(256)S(1)} %bitcast.178, f32[2048]{0:T(1024)S(1)} %add_rsqrt_fusion, bf16[2,1024,256]{2,1,0:T(8,128)(2,1)} %param.20, bf16[2,256,1024]{2,1,0:T(8,128)(2,1)} %param.19), kind=kOutput, calls=%fused_computation.72 | convolution fusion | flops 2168979456 | bytes 6300672 | tf_op jit(solution)/shard_map/dot_general | solution.py:90
  247.6 29.3 %all_to_all.8 = bf16[8,256,256]{2,1,0:T(8,128)(2,1)S(1)} all-to-all(bf16[8,256,256]{2,1,0:T(8,128)(2,1)S(1)} %bitcast.170), channel_id=1, replica_groups=mesh['groups'=2,'tm'=8,'sector'=2] {'tm'}, dimensions={0} | all-to-all | bytes 2097152 | tf_op jit(solution)/shard_map/all_to_all | solution.py:96
  (78 shorter events, 56.2 us)
Async XLA Ops:
  6.5 58.1 %reduce-scatter.2.cloned.1.call-start = ((), (), s32[]{:S(2)}) async-start(), calls=%async_computation.3 | async-start | bytes 3145728 | tf_op jit(solution)/shard_map/reduce_scatter | solution.py:109
  52.0 18.9 %copy-start.5 = (bf16[8,256]{1,0:T(8,128)(2,1)S(1)}, bf16[8,256]{1,0:T(8,128)(2,1)}, u32[]{:S(2)}) copy-start(bf16[8,256]{1,0:T(8,128)(2,1)} %param.15) | copy-start | bytes 12292
  52.0 18.9 %copy-start.6 = (f32[2,2,256]{2,1,0:T(2,128)S(1)}, f32[2,2,256]{2,1,0:T(2,128)}, u32[]{:S(2)}) copy-start(f32[2,2,256]{2,1,0:T(2,128)} %param.16) | copy-start | bytes 12292
  64.7 32.3 %all-to-all-start = ((bf16[1,8,256,256]{3,2,0,1:T(8,128)(2,1)}), bf16[1,8,256,256]{3,2,0,1:T(8,128)(2,1)S(1)}, u32[]{:S(2)}, u32[]{:S(2)}) async-start(bf16[1,8,256,256]{3,2,0,1:T(8,128)(2,1)} %bitcast.169), calls=%async_computation.1 | async-start | bytes 2097152 | tf_op jit(solution)/shard_map/all_to_all | solution.py:114
  96.9 1.0 copy-start
  158.7 6.3 %copy-start.1 = (bf16[1,8,256,256]{3,2,0,1:T(8,128)(2,1)S(1)}, bf16[1,8,256,256]{3,2,0,1:T(8,128)(2,1)}, u32[]{:S(2)}) copy-start(bf16[1,8,256,256]{3,2,0,1:T(8,128)(2,1)} %copy-done) | copy-start | bytes 3145732
  164.7 1.0 copy-start.4
  233.7 6.3 %copy-start.2 = (f32[2048,256]{1,0:T(8,128)S(1)}, f32[2048,256]{1,0:T(8,128)}, u32[]{:S(2)}) copy-start(f32[2048,256]{1,0:T(8,128)} %get-tuple-element.91) | copy-start | bytes 6291460
  242.0 37.6 %copy-start.3 = (bf16[3,3,256,256]{3,2,1,0:T(8,128)(2,1)S(1)}, bf16[3,3,256,256]{3,2,1,0:T(8,128)(2,1)}, u32[]{:S(2)}) copy-start(bf16[3,3,256,256]{3,2,1,0:T(8,128)(2,1)} %param.21) | copy-start | bytes 3538948
  277.0 2.7 collective-permute-start
  278.3 3.1 %collective-permute-start.1 = (bf16[1,1,64,256]{3,2,1,0:T(8,128)(2,1)S(1)}, bf16[1,1,64,256]{3,2,1,0:T(8,128)(2,1)S(1)}, u32[]{:S(2)}, u32[]{:S(2)}) collective-permute-start(bf16[1,1,64,256]{3,2,1,0:T(8,128)(2,1)S(1)} %get-tuple-element.81), channel_id=1, source_target_pairs={{1,0},{3,2},{5,4},{7,6},{9,8},{11,10},{13,12},{15,14},{17,16},{19,... | collective-permute-start | bytes 98312 | tf_op jit(solution)/shard_map/ppermute | solution.py:20
Sparse Core Ops, SparseCore 0:
  52.1 12.4 reduce-scatter.1
where the time goes:
time: 299 us; the launch traced here: 296 us
  local copies, waits for them, and re-layouts  101 us (34%)
  matrix products  73.3 us (25%)
  waiting for transfers between devices  40.3 us (13%)
  blocking collectives  29.3 us (10%)
  other arithmetic  28.7 us (10%)
  between operations  13.9 us (5%)
  starting transfers between devices  8.78 us (3%)
    unnamed x24, local copies, waits for them, and re-layouts  51.1 us
    all_to_all x1, blocking collectives, encode_return(): lax.all_to_all(encoded, 'tm', split_axis=0, concat_axis=1, tiled=True)  29.3 us
    all_to_all x1, waiting for transfers between devices, body(): lax.all_to_all(sectioned, 'tm', split_axis=1, concat_axis=0, tiled=True)  26 us
    reduce_sum x8, other arithmetic, one_block(): jnp.sum(jnp.where(matches, weights[:, None, :], jnp.zeros_like(weights[:,...  20 us
    dot_general x2, matrix products, encode_stack(): jnp.einsum('fchd,gchd->chfg', projected[:, :, 0], projected[:, :, 1], pre...  18 us
    dot_general x8, matrix products, one_block(): jnp.dot(matrix, features, preferred_element_type=jnp.float32)  15.7 us
    dot_general x2, matrix products, encode_stack(): jnp.einsum('chfg,gchd->fchd', soft_weights, projected[:, :, 2], preferred...  15.5 us
    convert_element_type x2, local copies, waits for them, and re-layouts, encode_stack(): (raised / jnp.sum(raised, axis=-1, keepdims=True)).astype(jnp.bfloat16)  12.8 us
  transfers between devices with their start and end apart: 4, of which 3 were waited for; matrix products, arithmetic and copies ran while one was open for 0% of the time, Pallas kernels for 0%

commit v1 on v0

--- a/solution.py
+++ b/solution.py
@@ -93,7 +93,10 @@
 
 def encode_return(tokens, weights):
     encoded = encode_stack(tokens, *weights)
-    return lax.all_to_all(encoded, "tm", split_axis=0, concat_axis=1, tiled=True)
+    return jnp.concatenate(
+        lax.all_to_all(jnp.stack(jnp.split(encoded, lax.axis_size("tm"), axis=0)), "tm", 0, 0),
+        axis=1,
+    )
 
 
 def body(

time: 299 us -> 313 us (1.047)
  local copies, waits for them, and re-layouts: 101 us -> 113 us
  matrix products: 73.3 us -> 77.3 us
  waiting for transfers between devices: 40.3 us -> 36.6 us
    convert_element_type x0 -> x2, local copies, waits for them, and re-layouts: none -> 3.37 us  [the longest x1 1.74 us: encode_stack(): tokens.astype(jnp.float32) + time_embed[:, None, :].astype(jnp.float32)]
    unnamed x24 -> x43, local copies, waits for them, and re-layouts: 51.1 us -> 53.4 us
  transfers between devices with their start and end apart: 4 -> 4, of which waited for: 3 -> 2; matrix products, arithmetic and copies ran while one was open for 0% -> 2% of each run, Pallas kernels for 0% -> 0%
where the time goes in v1:
time: 313 us; the launch traced here: 308 us
  local copies, waits for them, and re-layouts  113 us (36%)
  matrix products  77.3 us (25%)
  waiting for transfers between devices  36.6 us (12%)
  blocking collectives  29.5 us (9%)
  other arithmetic  27.9 us (9%)
  between operations  14.2 us (5%)
  starting transfers between devices  8.96 us (3%)
    unnamed x43, local copies, waits for them, and re-layouts  53.4 us
    all_to_all x1, blocking collectives, encode_return(): lax.all_to_all(jnp.stack(jnp.split(encoded, lax.axis_size('tm'), axis=0))...  29.5 us
    all_to_all x1, waiting for transfers between devices, body(): lax.all_to_all(sectioned, 'tm', split_axis=1, concat_axis=0, tiled=True)  23.9 us
    reduce_sum x8, other arithmetic, one_block(): jnp.sum(jnp.where(matches, weights[:, None, :], jnp.zeros_like(weights[:,...  20 us
    dot_general x2, matrix products, encode_stack(): jnp.einsum('fchd,gchd->chfg', projected[:, :, 0], projected[:, :, 1], pre...  18 us
    dot_general x8, matrix products, one_block(): jnp.dot(matrix, features, preferred_element_type=jnp.float32)  15.6 us
    dot_general x2, matrix products, encode_stack(): jnp.einsum('chfg,gchd->fchd', soft_weights, projected[:, :, 2], preferred...  15.5 us
    dot_general x2, matrix products, encode_stack(): jnp.dot(hidden_units, w_down[number], preferred_element_type=jnp.float32)  13.6 us
  transfers between devices with their start and end apart: 4, of which 2 were waited for; matrix products, arithmetic and copies ran while one was open for 2% of the time, Pallas kernels for 0%

profile of v1, /device:TPU:0, one launch (start us, length us, event | category | flops | bytes accessed | tf_op | source)
XLA Modules:
  0.0 308.2 jit_solution(12580949665610882996)
XLA Ops:
  6.5 44.5 %while.17 = (s32[]{:T(128)}, bf16[8,512,256]{2,1,0:T(8,128)(2,1)}, s32[1,16,512]{2,1,0:T(8,128)}, s32[8]{0:T(128)S(1)}, f32[16,512]{1,0:T(8,128)}, /*index=5*/bf16[512,256]{1,0:T(8,128)(2,1)}, s32[]{:T(128)}) while((s32[]{:T(128)}, bf16[8,512,256]{2,1,0:T(8,128)(2,1)}, s32[1,16,512]{2,1,0:T(8,128)}, s32[8]{0:T(128)S(1)}, f32[16,512]{1,0:T(8,128)}, ...), condition=%wide.region_2.3_spmd, body=%wide.region_0.2_spmd.sunk | while | flops 146670080 | bytes 1643101 | solution.py:46
  18.8 2.5 select_reduce_fusion.2
  24.3 2.5 select_reduce_fusion.2
  51.1 12.6 %reduce-scatter.2.cloned.1.call-done = bf16[1,2048,256]{2,1,0:T(8,128)(2,1)} async-done(((bf16[1,4096,256]{2,1,0:T(8,128)(2,1)}), bf16[1,2048,256]{2,1,0:T(8,128)(2,1)}) %reduce-scatter.2.cloned.1.call-update) | async-done | bytes 1048592 | tf_op jit(solution)/shard_map/reduce_scatter | solution.py:112
  66.0 6.4 %all-to-all-start = ((bf16[1,8,256,256]{2,3,0,1:T(8,128)(2,1)}), bf16[1,8,256,256]{2,3,0,1:T(8,128)(2,1)S(1)}, u32[]{:S(2)}, u32[]{:S(2)}) async-start(bf16[1,8,256,256]{2,3,0,1:T(8,128)(2,1)} %copy.94), calls=%async_computation.1 | async-start | bytes 2097152 | tf_op jit(solution)/shard_map/all_to_all | solution.py:117
  74.5 23.9 %all-to-all-done = bf16[1,8,256,256]{2,3,0,1:T(8,128)(2,1)S(1)} async-done(((bf16[1,8,256,256]{2,3,0,1:T(8,128)(2,1)}), bf16[1,8,256,256]{2,3,0,1:T(8,128)(2,1)S(1)}, u32[]{:S(2)}, u32[]{:S(2)}) %all-to-all-start) | async-done | bytes 1048608 | tf_op jit(solution)/shard_map/all_to_all | solution.py:117
  101.4 3.0 copy.98
  104.4 3.0 copy.124
  107.6 7.2 %copy.119 = bf16[8,256,1,8,32]{4,0,3,1,2:T(8,128)(2,1)} copy(bf16[8,256,1,8,32]{1,0,4,3,2:T(8,128)(2,1)S(1)} %get-tuple-element.69) | data formatting | bytes 2097152
  114.8 7.2 %copy.120 = bf16[8,256,1,8,32]{4,0,3,1,2:T(8,128)(2,1)} copy(bf16[8,256,1,8,32]{1,0,4,3,2:T(8,128)(2,1)S(1)} %get-tuple-element.70) | data formatting | bytes 2097152
  121.9 9.0 %fusion.26 = f32[256,8,8,8]{2,3,1,0:T(8,128)} fusion(bf16[8,256,1,8,32]{4,0,3,1,2:T(8,128)(2,1)} %copy.120, bf16[8,256,1,8,32]{4,0,3,1,2:T(8,128)(2,1)} %copy.119), kind=kOutput, calls=%fused_computation.31 | convolution fusion | flops 8388608 | bytes 2621440 | tf_op jit(solution)/shard_map/fchd,gchd->chfg/dot_general | solution.py:70
  131.0 6.4 %copy.102 = f32[256,8,8,8]{0,3,2,1:T(8,128)S(1)} copy(f32[256,8,8,8]{2,3,1,0:T(8,128)} %fusion.26) | data formatting | bytes 1048576 | tf_op jit(solution)/shard_map/fchd,gchd->chfg/dot_general | solution.py:70
  138.4 6.4 %copy.103 = bf16[256,8,8,8]{3,2,1,0:T(8,128)(2,1)} copy(bf16[256,8,8,8]{0,3,2,1:T(8,128)(2,1)S(1)} %divide_convert_fusion.1) | data formatting | bytes 524288 | tf_op jit(solution)/shard_map/convert_element_type | solution.py:79
  144.8 7.4 %copy.118 = bf16[8,256,1,8,32]{4,0,3,1,2:T(8,128)(2,1)} copy(bf16[8,256,1,8,32]{1,0,4,3,2:T(8,128)(2,1)S(1)} %get-tuple-element.68) | data formatting | bytes 2097152
  152.2 7.7 %convert_bitcast_fusion.1 = bf16[8,256,8,32]{3,0,2,1:T(8,128)(2,1)} fusion(bf16[256,8,8,8]{3,2,1,0:T(8,128)(2,1)} %copy.103, bf16[8,256,1,8,32]{4,0,3,1,2:T(8,128)(2,1)} %copy.118), kind=kOutput, calls=%fused_computation.37 | convolution fusion | flops 8912896 | bytes 2359296 | tf_op jit(solution)/shard_map/chfg,gchd->fchd/dot_general | solution.py:80
  159.9 6.8 %copy.104 = bf16[8,256,8,32]{1,0,3,2:T(8,128)(2,1)} copy(bf16[8,256,8,32]{3,0,2,1:T(8,128)(2,1)} %convert_bitcast_fusion.1) | data formatting | bytes 2097152 | tf_op jit(solution)/shard_map/convert_element_type | solution.py:82
  166.7 2.7 copy.125
  171.1 3.8 %multiply_reduce_fusion.2 = (f32[2048]{0:T(1024)S(1)}, f32[2048,256]{0,1:T(8,128)}) fusion(bf16[2048,256]{0,1:T(8,128)(2,1)} %bitcast.196, bf16[2,256,256]{2,1,0:T(8,128)(2,1)S(1)} %copy-done.10, f32[2048,256]{0,1:T(8,128)} %copy.116, f32[2048,256]{0,1:T(8,128)S(1)} %copy-done.2), kind=kOutput, calls=%fused_computation.81 | convolution fusion | flops 270530560 | bytes 7479296 | tf_op jit(solution)/shard_map/dot_general | solution.py:84
  174.9 7.5 %multiply_reduce_fusion.1 = (f32[2048]{0:T(1024)S(1)}, f32[2048,256]{0,1:T(8,128)}) fusion(f32[2048,256]{0,1:T(8,128)} %get-tuple-element.89, bf16[2,1024,256]{2,1,0:T(8,128)(2,1)} %param.20, f32[256]{0:T(256)S(1)} %bitcast.209, f32[2048]{0:T(1024)S(1)} %add_rsqrt_fusion.2, bf16[2,256,1024]{2,1,0:T(8,128)(2,1)} %param.19), kind=kOutput, calls=%fused_computation.79 | convolution fusion | flops 2169501696 | bytes 7357440 | tf_op jit(solution)/shard_map/dot_general | solution.py:90
  182.4 2.7 convolution_convert_fusion.1
  185.2 3.1 %copy.105 = bf16[2048,768]{0,1:T(8,128)(2,1)} copy(bf16[2048,768]{1,0:T(8,128)(2,1)S(1)} %convolution_convert_fusion.1) | data formatting | bytes 6291456 | tf_op jit(solution)/shard_map/convert_element_type | solution.py:66
  188.4 3.0 copy.126
  191.5 7.2 %copy.122 = bf16[8,256,1,8,32]{4,0,3,1,2:T(8,128)(2,1)} copy(bf16[8,256,1,8,32]{1,0,4,3,2:T(8,128)(2,1)S(1)} %get-tuple-element.66) | data formatting | bytes 2097152
  198.7 7.2 %copy.123 = bf16[8,256,1,8,32]{4,0,3,1,2:T(8,128)(2,1)} copy(bf16[8,256,1,8,32]{1,0,4,3,2:T(8,128)(2,1)S(1)} %get-tuple-element.67) | data formatting | bytes 2097152
  205.9 9.0 %fusion.21 = f32[256,8,8,8]{2,3,1,0:T(8,128)} fusion(bf16[8,256,1,8,32]{4,0,3,1,2:T(8,128)(2,1)} %copy.123, bf16[8,256,1,8,32]{4,0,3,1,2:T(8,128)(2,1)} %copy.122), kind=kOutput, calls=%fused_computation.26 | convolution fusion | flops 8388608 | bytes 2621440 | tf_op jit(solution)/shard_map/fchd,gchd->chfg/dot_general | solution.py:70
  214.9 6.4 %copy.109 = f32[256,8,8,8]{0,3,2,1:T(8,128)S(1)} copy(f32[256,8,8,8]{2,3,1,0:T(8,128)} %fusion.21) | data formatting | bytes 1048576 | tf_op jit(solution)/shard_map/fchd,gchd->chfg/dot_general | solution.py:70
  222.4 6.4 %copy.110 = bf16[256,8,8,8]{3,2,1,0:T(8,128)(2,1)} copy(bf16[256,8,8,8]{0,3,2,1:T(8,128)(2,1)S(1)} %divide_convert_fusion) | data formatting | bytes 524288 | tf_op jit(solution)/shard_map/convert_element_type | solution.py:79
  228.8 7.4 %copy.121 = bf16[8,256,1,8,32]{4,0,3,1,2:T(8,128)(2,1)} copy(bf16[8,256,1,8,32]{1,0,4,3,2:T(8,128)(2,1)S(1)} %get-tuple-element.65) | data formatting | bytes 2097152
  236.2 7.7 %convert_bitcast_fusion = bf16[8,256,8,32]{3,0,2,1:T(8,128)(2,1)} fusion(bf16[256,8,8,8]{3,2,1,0:T(8,128)(2,1)} %copy.110, bf16[8,256,1,8,32]{4,0,3,1,2:T(8,128)(2,1)} %copy.121), kind=kOutput, calls=%fused_computation.36 | convolution fusion | flops 8912896 | bytes 2359296 | tf_op jit(solution)/shard_map/chfg,gchd->fchd/dot_general | solution.py:80
  243.9 6.0 %copy.111 = bf16[8,256,8,32]{1,0,3,2:T(8,128)(2,1)S(1)} copy(bf16[8,256,8,32]{3,0,2,1:T(8,128)(2,1)} %convert_bitcast_fusion) | data formatting | bytes 2097152 | tf_op jit(solution)/shard_map/convert_element_type | solution.py:82
  252.1 6.1 %fusion.70 = bf16[2048,256]{0,1:T(8,128)(2,1)S(1)} fusion(f32[2048,256]{0,1:T(8,128)} %get-tuple-element.95, f32[256]{0:T(256)S(1)} %bitcast.208, f32[2048]{0:T(1024)S(1)} %add_rsqrt_fusion, bf16[2,1024,256]{2,1,0:T(8,128)(2,1)} %param.20, bf16[2,256,1024]{2,1,0:T(8,128)(2,1)} %param.19), kind=kOutput, calls=%fused_computation.72 | convolution fusion | flops 2168979456 | bytes 6300672 | tf_op jit(solution)/shard_map/dot_general | solution.py:90
  258.5 29.5 %all_to_all.14 = bf16[8,1,256,256]{2,3,1,0:T(8,128)(2,1)S(1)} all-to-all(bf16[8,1,256,256]{2,3,1,0:T(8,128)(2,1)S(1)} %fusion.122), channel_id=1, replica_groups=mesh['groups'=2,'tm'=8,'sector'=2] {'tm'}, dimensions={0} | all-to-all | bytes 2097152 | tf_op jit(solution)/shard_map/all_to_all | solution.py:97
  (104 shorter events, 66.1 us)
Async XLA Ops:
  6.5 57.2 %reduce-scatter.2.cloned.1.call-start = ((), (), s32[]{:S(2)}) async-start(), calls=%async_computation.3 | async-start | bytes 3145728 | tf_op jit(solution)/shard_map/reduce_scatter | solution.py:112
  51.1 21.3 %copy-start.11 = (bf16[8,256]{1,0:T(8,128)(2,1)S(1)}, bf16[8,256]{1,0:T(8,128)(2,1)}, u32[]{:S(2)}) copy-start(bf16[8,256]{1,0:T(8,128)(2,1)} %param.15) | copy-start | bytes 12292
  66.0 32.4 %all-to-all-start = ((bf16[1,8,256,256]{2,3,0,1:T(8,128)(2,1)}), bf16[1,8,256,256]{2,3,0,1:T(8,128)(2,1)S(1)}, u32[]{:S(2)}, u32[]{:S(2)}) async-start(bf16[1,8,256,256]{2,3,0,1:T(8,128)(2,1)} %copy.94), calls=%async_computation.1 | async-start | bytes 2097152 | tf_op jit(solution)/shard_map/all_to_all | solution.py:117
  72.4 2.1 copy-start.12
  98.9 1.0 copy-start
  98.9 1.5 copy-start.6
  159.9 9.5 %copy-start.1 = (bf16[1,8,256,256]{3,2,1,0:T(8,128)(2,1)S(1)}, bf16[1,8,256,256]{3,2,1,0:T(8,128)(2,1)}, u32[]{:S(2)}) copy-start(bf16[1,8,256,256]{3,2,1,0:T(8,128)(2,1)} %copy-done) | copy-start | bytes 3145732
  166.7 4.4 %copy-start.2 = (f32[2048,256]{0,1:T(8,128)S(1)}, f32[2048,256]{0,1:T(8,128)}, u32[]{:S(2)}) copy-start(f32[2048,256]{0,1:T(8,128)} %copy.117) | copy-start | bytes 6291460
  166.7 4.4 %copy-start.10 = (bf16[2,256,256]{2,1,0:T(8,128)(2,1)S(1)}, bf16[2,256,256]{2,1,0:T(8,128)(2,1)}, u32[]{:S(2)}) copy-start(bf16[2,256,256]{2,1,0:T(8,128)(2,1)} %param.18) | copy-start | bytes 786436
  243.9 6.3 %copy-start.3 = (f32[2048,256]{0,1:T(8,128)S(1)}, f32[2048,256]{0,1:T(8,128)}, u32[]{:S(2)}) copy-start(f32[2048,256]{0,1:T(8,128)} %get-tuple-element.91) | copy-start | bytes 6291460
  258.3 32.8 %copy-start.5 = (bf16[3,3,256,256]{3,2,1,0:T(8,128)(2,1)S(1)}, bf16[3,3,256,256]{3,2,1,0:T(8,128)(2,1)}, u32[]{:S(2)}) copy-start(bf16[3,3,256,256]{3,2,1,0:T(8,128)(2,1)} %param.21) | copy-start | bytes 3538948
  288.5 5.3 %collective-permute-start = (bf16[1,1,64,256]{3,2,1,0:T(8,128)(2,1)S(1)}, bf16[1,1,64,256]{3,2,1,0:T(8,128)(2,1)S(1)}, u32[]{:S(2)}, u32[]{:S(2)}) collective-permute-start(bf16[1,1,64,256]{3,2,1,0:T(8,128)(2,1)S(1)} %get-tuple-element.80), channel_id=1, source_target_pairs={{0,1},{2,3},{4,5},{6,7},{8,9},{10,11},{12,13},{14,15},{16,17},{18,... | collective-permute-start | bytes 98312 | tf_op jit(solution)/shard_map/ppermute | solution.py:18
  289.8 4.0 %collective-permute-start.1 = (bf16[1,1,64,256]{3,2,1,0:T(8,128)(2,1)S(1)}, bf16[1,1,64,256]{3,2,1,0:T(8,128)(2,1)S(1)}, u32[]{:S(2)}, u32[]{:S(2)}) collective-permute-start(bf16[1,1,64,256]{3,2,1,0:T(8,128)(2,1)S(1)} %get-tuple-element.81), channel_id=1, source_target_pairs={{1,0},{3,2},{5,4},{7,6},{9,8},{11,10},{13,12},{15,14},{17,16},{19,... | collective-permute-start | bytes 98312 | tf_op jit(solution)/shard_map/ppermute | solution.py:20
  294.5 1.1 copy-start.9
  295.6 1.6 copy-start.8
  297.2 1.6 copy-start.4
  297.2 1.6 copy-start.7
Sparse Core Ops, SparseCore 0:
  51.2 12.4 reduce-scatter.1
